TPU v7x, 32 devices: a whole 2x2x4 slice. The times are simulated.
32 devices in a mesh: groups: 2 (over y), ctx: 4 (over z), role: 2 (over x), seq: 2 (over core).
Axes of the slice: x: 2, y: 2, z: 4, core: 2. Of those that a mesh axis runs over, the one named last changes fastest.
Arguments:
- queries: bfloat16 [32, 128, 576], P(('groups', 'role', 'seq'), 'ctx'), parts along dimension 0, may hold values from -24 to 24
- cache: bfloat16 [16, 4096, 576], P(('groups', 'role', 'seq'), 'ctx'), parts along dimension 0, may hold values from -4 to 4
- lengths: int32 [16], P(('groups', 'role', 'seq')), parts along dimension 0, may hold values from 4 to 4096, as said below
- positions: int32 [32], P(('groups', 'role', 'seq')), parts along dimension 0, may hold values from 0 to 4098, as said below
- value_up_weight: bfloat16 [128, 512, 128], P('ctx', ('role', 'seq')), may hold values from -0.25 to 0.25
- out_proj: bfloat16 [16384, 7168], P('ctx', ('role', 'seq')), may hold values from -0.046875 to 0.046875
- residual: bfloat16 [32, 7168], P('groups', ('role', 'seq')), parts along dimension 0, may hold values from -4 to 4
- norm_gain: float32 [7168], P(('role', 'seq')), may hold values from 0.5 to 1.5
- gate_weight: bfloat16 [7168, 9216], P(('role', 'seq'), 'ctx'), may hold values from -0.0625 to 0.0625
- up_weight: bfloat16 [7168, 9216], P(('role', 'seq'), 'ctx'), may hold values from -0.0625 to 0.0625
- down_weight: bfloat16 [9216, 7168], P('ctx', ('role', 'seq')), may hold values from -0.0625 to 0.0625
Outputs:
- layer_out: bfloat16 [32, 7168], P(('groups', 'ctx'), ('role', 'seq')), parts along dimension 0
There are 2 independent parts, one for each index of `groups`. A program takes and returns all parts, laid end to end along the dimension named above; an argument that names none is the same for every part. Nothing has to cross between parts.
Inputs may be any that keep to these rules, and one draw needn't show every extreme that they name: `lengths`: every sequence has at least 4 cached positions, and in every draw some sequence has all 4096. positions[r] lies between lengths[r // 2] - 4 and lengths[r // 2] + 2.
All inputs are finite; a program needn't handle non-finite values.
Results may differ from a plain program's by a relative error of at most 0.013.
Values may be sent and summed in bfloat16 or wider, within the bound.
A program may use at most 128 MiB of HBM per device.

v0:
```python
import jax
import jax.numpy as jnp
from jax import lax
from jax.sharding import PartitionSpec as P

D = 7168
HEADS = 128
LATENT = 512
ROPE = 64
VDIM = 128
MTP = 2
softmax_scale = 0.07216878364870323
epsilon = 1e-06


def settle_heads(pieces):
    maxima, totals, partial_value = pieces
    highest = jnp.max(maxima, axis=0)
    factor = jnp.exp(maxima - highest[None])
    denom = jnp.sum(factor * totals, axis=0)
    numer = jnp.sum(factor[..., None] * partial_value, axis=0)
    return (numer / denom[..., None]).astype(jnp.bfloat16)


def per_device(
    queries,
    cache,
    lengths,
    positions,
    value_up_weight,
    out_proj,
    residual,
    norm_gain,
    gate_weight,
    up_weight,
    down_weight,
):
    all_heads = lax.all_gather(queries, "ctx", axis=1, tiled=True)
    heads_here = queries.shape[1]
    width = LATENT + ROPE
    context_local = cache.shape[1]
    seq_here = cache.shape[0]
    offset = lax.axis_index("ctx") * context_local
    places = offset + jnp.arange(context_local, dtype=jnp.int32)
    maxima_list = []
    totals_list = []
    partial_list = []
    for number in range(seq_here):
        rows_pair = all_heads[MTP * number : MTP * (number + 1)].reshape(MTP * HEADS, width)
        keys_here = cache[number]
        limits = jnp.repeat(positions[MTP * number : MTP * (number + 1)], HEADS)
        length = lengths[number]

        def compute_block(rows_pair=rows_pair, keys_here=keys_here, limits=limits, length=length):
            scores = (
                jnp.dot(rows_pair, keys_here.T, preferred_element_type=jnp.float32) * softmax_scale
            )
            live = (places[None, :] < length) & (places[None, :] <= limits[:, None])
            block_max = jnp.max(jnp.where(live, scores, jnp.float32(-1e30)), axis=-1)
            probs = jnp.exp(
                jnp.where(live, scores - block_max[:, None], jnp.float32(-1e30))
            ).astype(jnp.bfloat16)
            block_weight_sum = jnp.sum(probs.astype(jnp.float32), axis=-1)
            block_out = jnp.dot(probs, keys_here[:, :LATENT], preferred_element_type=jnp.float32)
            return (block_max, block_weight_sum, block_out)

        block_max, block_weight_sum, block_out = compute_block()
        maxima_list.append(block_max.reshape(MTP, HEADS))
        totals_list.append(block_weight_sum.reshape(MTP, HEADS))
        partial_list.append(block_out.reshape(MTP, HEADS, LATENT))
    maxima = jnp.concatenate(maxima_list, axis=0)
    totals = jnp.concatenate(totals_list, axis=0)
    partial_value = jnp.concatenate(partial_list, axis=0)
    attended_values = settle_heads(
        (
            lax.all_to_all(maxima[None], "ctx", split_axis=2, concat_axis=0, tiled=True),
            lax.all_to_all(totals[None], "ctx", split_axis=2, concat_axis=0, tiled=True),
            lax.all_to_all(partial_value[None], "ctx", split_axis=2, concat_axis=0, tiled=True),
        )
    )
    mixed = jnp.einsum(
        "nut,utc->nuc",
        attended_values,
        lax.all_gather(value_up_weight, ("role", "seq"), axis=1, tiled=True),
        preferred_element_type=jnp.float32,
    )
    value_vectors = mixed.astype(jnp.bfloat16).reshape(attended_values.shape[0], heads_here * VDIM)
    per_head_terms = jnp.dot(
        lax.all_gather(value_vectors, ("role", "seq"), axis=0, tiled=True),
        out_proj,
        preferred_element_type=jnp.float32,
    )
    attn_out = lax.psum(per_head_terms, "ctx")
    resid = residual.astype(jnp.float32) + attn_out
    sumsq = lax.psum(jnp.sum(resid * resid, axis=1), ("role", "seq"))
    normed = (resid * lax.rsqrt(sumsq / D + epsilon)[:, None] * norm_gain[None, :]).astype(
        jnp.bfloat16
    )
    gate_term = jnp.dot(normed, gate_weight, preferred_element_type=jnp.float32)
    up_term = jnp.dot(normed, up_weight, preferred_element_type=jnp.float32)
    gate, up = lax.psum((gate_term, up_term), ("role", "seq"))
    hidden = (jax.nn.silu(gate) * up).astype(jnp.bfloat16)
    rows_here = resid.shape[0] // lax.axis_size("ctx")
    ffn_rows = lax.psum_scatter(
        jnp.dot(hidden, down_weight, preferred_element_type=jnp.float32),
        "ctx",
        scatter_dimension=0,
        tiled=True,
    )
    base_rows = lax.dynamic_slice_in_dim(resid, lax.axis_index("ctx") * rows_here, rows_here, 0)
    return (base_rows + ffn_rows).astype(jnp.bfloat16)


def solution(mesh):
    placed = (
        P(("groups", "role", "seq"), "ctx", None),
        P(("groups", "role", "seq"), "ctx", None),
        P(("groups", "role", "seq")),
        P(("groups", "role", "seq")),
        P("ctx", ("role", "seq"), None),
        P("ctx", ("role", "seq")),
        P("groups", ("role", "seq")),
        P(("role", "seq")),
        P(("role", "seq"), "ctx"),
        P(("role", "seq"), "ctx"),
        P("ctx", ("role", "seq")),
    )
    return jax.shard_map(
        per_device,
        mesh=mesh,
        in_specs=placed,
        out_specs=P(("groups", "ctx"), ("role", "seq")),
        check_vma=False,
    )
```

profile of v0, /device:TPU:0, one launch (start us, length us, event | category | flops | bytes accessed | tf_op | source)
XLA Modules:
  0.0 227.1 jit_solution(11326140525146923370)
XLA Ops:
  6.5 0.7 all-gather.3.cloned.1.call-update
  7.3 1.3 fusion.19
  8.6 1.3 fusion.12
  9.9 19.9 %all_gather.9 = bf16[4,128,576]{2,1,0:T(8,128)(2,1)S(1)} all-gather(bf16[4,32,576]{2,1,0:T(8,128)(2,1)} %param.11), channel_id=1, replica_groups=mesh['groups'=2,'ctx'=4,'role'=2,'seq'=2] {'ctx'}, dimensions={1}, use_global_device_ids=true | all-gather | bytes 737280 | tf_op jit(solution)/shard_map/all_gather | solution.py:38
  29.8 0.8 fusion.20
  30.7 1.8 convolution_multiply_fusion
  32.6 0.9 select_reduce_fusion.1
  33.5 0.9 convert_reduce_fusion.1
  35.1 0.8 reduce.1
  35.9 0.7 reshape.68
  36.6 3.8 %all-to-all-start.2 = ((f32[4,1,128]{2,1,0:T(1,128)}), f32[4,1,128]{2,1,0:T(1,128)S(1)}, u32[]{:S(2)}, u32[]{:S(2)}) async-start(f32[4,1,128]{2,1,0:T(1,128)} %reshape.68), calls=%async_computation.2 | async-start | bytes 4096 | tf_op jit(solution)/shard_map/all_to_all | solution.py:77
  41.7 0.8 reduce.3
  42.5 0.7 reshape.66
  44.0 1.9 all-to-all-done.2
  45.9 3.2 %all-to-all-start = ((f32[4,1,128]{2,1,0:T(1,128)}), f32[4,1,128]{2,1,0:T(1,128)S(1)}, u32[]{:S(2)}, u32[]{:S(2)}) async-start(f32[4,1,128]{2,1,0:T(1,128)} %reshape.66), calls=%async_computation | async-start | bytes 4096 | tf_op jit(solution)/shard_map/all_to_all | solution.py:76
  49.1 1.4 maximum_bitcast_fusion
  50.6 4.1 %all-to-all-done = f32[4,1,128]{2,1,0:T(1,128)S(1)} async-done(((f32[4,1,128]{2,1,0:T(1,128)}), f32[4,1,128]{2,1,0:T(1,128)S(1)}, u32[]{:S(2)}, u32[]{:S(2)}) %all-to-all-start) | async-done | bytes 2080 | tf_op jit(solution)/shard_map/all_to_all | solution.py:76
  54.7 3.5 %all-to-all-start.1 = ((f32[1,4,128,512]{3,1,0,2:T(4,128)}), f32[1,4,128,512]{3,1,0,2:T(4,128)S(1)}, u32[]{:S(2)}, u32[]{:S(2)}) async-start(f32[1,4,128,512]{3,1,0,2:T(4,128)} %maximum_bitcast_fusion), calls=%async_computation.1 | async-start | bytes 2097152 | tf_op jit(solution)/shard_map/all_to_all | solution.py:78
  59.2 0.7 reduce.4
  60.1 18.8 %all-to-all-done.1 = f32[1,4,128,512]{3,1,0,2:T(4,128)S(1)} async-done(((f32[1,4,128,512]{3,1,0,2:T(4,128)}), f32[1,4,128,512]{3,1,0,2:T(4,128)S(1)}, u32[]{:S(2)}, u32[]{:S(2)}) %all-to-all-start.1) | async-done | bytes 1048608 | tf_op jit(solution)/shard_map/all_to_all | solution.py:78
  79.4 2.8 %fusion = bf16[1,4,4096]{2,1,0:T(4,128)(2,1)S(1)} fusion(bf16[32,512,128]{2,1,0:T(8,128)(2,1)} %all-gather.3.cloned.1.call-done, bf16[4,32,512]{2,1,0:T(8,128)(2,1)S(1)} %divide_convert_fusion), kind=kOutput, calls=%fused_computation.5 | convolution fusion | flops 16793600 | bytes 4358144 | tf_op jit(solution)/shard_map/nut,utc->nuc/dot_general | solution.py:81
  82.2 5.4 %all-gather = bf16[4,4,4096]{2,1,0:T(4,128)(2,1)S(1)} all-gather(bf16[1,4,4096]{2,1,0:T(4,128)(2,1)S(1)} %fusion), channel_id=1, replica_groups=mesh['groups'=2,'ctx'=4,'role'=2,'seq'=2] {'role','seq'}, dimensions={0}, use_global_device_ids=true | all-gather | bytes 163840 | tf_op jit(solution)/shard_map/all_gather | solution.py:89
  87.7 7.8 %fusion.21 = f32[16,1792]{1,0:T(8,128)} fusion(bf16[16,4096]{1,0:T(8,128)(2,1)S(1)} %reshape.63, bf16[4096,1792]{1,0:T(8,128)(2,1)} %param.16), kind=kOutput, calls=%fused_computation.50 | convolution fusion | flops 234881024 | bytes 14925824 | tf_op jit(solution)/shard_map/dot_general | solution.py:88
  95.6 33.5 %all-reduce.6.cloned.1.call-done = f32[16,1792]{1,0:T(8,128)} async-done(((f32[16,1792]{1,0:T(8,128)}), f32[16,1792]{1,0:T(8,128)}) %all-reduce.6.cloned.1.call-update) | async-done | bytes 114704 | tf_op jit(solution)/shard_map/psum | solution.py:93
  129.1 1.0 multiply_reduce_fusion
  130.1 5.7 %psum.29 = f32[16]{0:T(128)S(1)} all-reduce(f32[16]{0:T(128)S(1)} %get-tuple-element.9), channel_id=1, replica_groups=mesh['groups'=2,'ctx'=4,'role'=2,'seq'=2] {'role','seq'}, use_global_device_ids=true, to_apply=%region_9.10 | all-reduce | flops 16 | bytes 128 | tf_op jit(solution)/shard_map/psum | solution.py:95
  135.8 5.2 %fusion.16 = f32[16,2304]{1,0:T(8,128)} fusion(bf16[1792,2304]{1,0:T(8,128)(2,1)} %param.19, f32[16,1792]{1,0:T(8,128)S(1)} %get-tuple-element.10, f32[1792]{0:T(1024)S(1)} %copy-done.1, f32[16]{0:T(128)S(1)} %add_rsqrt_fusion), kind=kOutput, calls=%fused_computation.46 | convolution fusion | flops 132206592 | bytes 8526912 | tf_op jit(solution)/shard_map/dot_general | solution.py:99
  141.1 5.3 %fusion.15 = f32[16,2304]{1,0:T(8,128)} fusion(bf16[1792,2304]{1,0:T(8,128)(2,1)} %param.20, f32[16,1792]{1,0:T(8,128)S(1)} %get-tuple-element.10, f32[1792]{0:T(1024)S(1)} %copy-done.1, f32[16]{0:T(128)S(1)} %add_rsqrt_fusion), kind=kOutput, calls=%fused_computation.45 | convolution fusion | flops 132206592 | bytes 8526912 | tf_op jit(solution)/shard_map/dot_general | solution.py:100
  146.4 32.9 %all-reduce.10.cloned.1.call-done = (f32[16,2304]{1,0:T(8,128)}, f32[16,2304]{1,0:T(8,128)}) async-done(((f32[16,2304]{1,0:T(8,128)}, f32[16,2304]{1,0:T(8,128)}), (f32[16,2304]{1,0:T(8,128)}, f32[16,2304]{1,0:T(8,128)})) %all-reduce.10.cloned.1.call-update) | async-done | bytes 294928 | tf_op jit(solution)/shard_map/psum | solution.py:101
  179.2 5.4 %fusion.7 = f32[16,1792]{1,0:T(8,128)} fusion(bf16[2304,1792]{1,0:T(8,128)(2,1)} %param.21, f32[16,2304]{1,0:T(8,128)} %get-tuple-element.7, f32[16,2304]{1,0:T(8,128)} %get-tuple-element.8), kind=kOutput, calls=%fused_computation.27 | convolution fusion | flops 132341760 | bytes 8667136 | tf_op jit(solution)/shard_map/dot_general | solution.py:105
  185.9 33.3 %all-reduce.8.cloned.1.call-done = f32[16,1792]{1,0:T(8,128)} async-done(((f32[16,1792]{1,0:T(8,128)}), f32[16,1792]{1,0:T(8,128)}) %all-reduce.8.cloned.1.call-update) | async-done | bytes 114704
  219.2 1.4 fusion.9
  (41 shorter events, 5.4 us)
Async XLA Ops:
  6.5 26.1 %copy-start = (bf16[2,1024,576]{1,2,0:T(8,128)(2,1)S(1)}, bf16[2,1024,576]{1,2,0:T(8,128)(2,1)}, u32[]{:S(2)}) copy-start(bf16[2,1024,576]{1,2,0:T(8,128)(2,1)} %param.12) | copy-start | bytes 7077892
  6.5 72.8 %all-gather.3.cloned.1.call-start = ((), (), s32[]{:S(2)}) async-start(), calls=%async_computation.3 | async-start | bytes 5242880 | tf_op jit(solution)/shard_map/all_gather | solution.py:84
  36.6 9.3 %all-to-all-start.2 = ((f32[4,1,128]{2,1,0:T(1,128)}), f32[4,1,128]{2,1,0:T(1,128)S(1)}, u32[]{:S(2)}, u32[]{:S(2)}) async-start(f32[4,1,128]{2,1,0:T(1,128)} %reshape.68), calls=%async_computation.2 | async-start | bytes 4096 | tf_op jit(solution)/shard_map/all_to_all | solution.py:77
  45.9 8.8 %all-to-all-start = ((f32[4,1,128]{2,1,0:T(1,128)}), f32[4,1,128]{2,1,0:T(1,128)S(1)}, u32[]{:S(2)}, u32[]{:S(2)}) async-start(f32[4,1,128]{2,1,0:T(1,128)} %reshape.66), calls=%async_computation | async-start | bytes 4096 | tf_op jit(solution)/shard_map/all_to_all | solution.py:76
  54.7 24.2 %all-to-all-start.1 = ((f32[1,4,128,512]{3,1,0,2:T(4,128)}), f32[1,4,128,512]{3,1,0,2:T(4,128)S(1)}, u32[]{:S(2)}, u32[]{:S(2)}) async-start(f32[1,4,128,512]{3,1,0,2:T(4,128)} %maximum_bitcast_fusion), calls=%async_computation.1 | async-start | bytes 2097152 | tf_op jit(solution)/shard_map/all_to_all | solution.py:78
  58.2 70.9 %all-reduce.6.cloned.1.call-start = ((), (), s32[]{:S(2)}) async-start(), calls=%async_computation.4 | async-start | bytes 229376 | tf_op jit(solution)/shard_map/psum | solution.py:93
  87.7 41.4 %copy-start.2 = (bf16[16,1792]{1,0:T(8,128)(2,1)S(1)}, bf16[16,1792]{1,0:T(8,128)(2,1)}, u32[]{:S(2)}) copy-start(bf16[16,1792]{1,0:T(8,128)(2,1)} %param.17) | copy-start | bytes 172036
  87.7 48.1 %copy-start.1 = (f32[1792]{0:T(1024)S(1)}, f32[1792]{0:T(1024)}, u32[]{:S(2)}) copy-start(f32[1792]{0:T(1024)} %param.18) | copy-start | bytes 21508
  95.6 83.7 %all-reduce.10.cloned.1.call-start = ((), (), s32[]{:S(2)}) async-start(), calls=%async_computation.6 | async-start | bytes 589824 | tf_op jit(solution)/shard_map/psum | solution.py:101
  146.3 72.8 %all-reduce.8.cloned.1.call-start = ((), (), s32[]{:S(2)}) async-start(), calls=%async_computation.5 | async-start | bytes 229376
  179.2 5.4 %copy-start.3 = (u32[32]{0:T(128)S(1)}, u32[32]{0:T(128)}, u32[]{:S(2)}) copy-start(u32[32]{0:T(128)} %constant.35) | copy-start | bytes 388
Sparse Core Ops, SparseCore 0:
  8.9 37.1 all-gather.2
  95.7 33.3 all-reduce.5
  146.4 32.7 all-reduce.9
  184.8 34.3 all-reduce.7
where the time goes:
time: 228 us; the launch traced here: 227 us
  waiting for transfers between devices  125 us (55%)
  blocking collectives  31 us (14%)
  matrix products  30.3 us (13%)
  between operations  14 us (6%)
  starting transfers between devices  10.7 us (5%)
  other arithmetic  9.47 us (4%)
  local copies, waits for them, and re-layouts  6.56 us (3%)
    unnamed x5, waiting for transfers between devices  34 us
    psum x1, waiting for transfers between devices, per_device(): attn_out = lax.psum(per_head_terms, 'ctx')  33.5 us
    psum x1, waiting for transfers between devices, per_device(): gate, up = lax.psum((gate_term, up_term), ('role', 'seq'))  32.9 us
    all_gather x1, blocking collectives, per_device(): all_heads = lax.all_gather(queries, 'ctx', axis=1, tiled=True)  19.9 us
    all_to_all x1, waiting for transfers between devices, per_device(): lax.all_to_all(partial_value[None], 'ctx', split_axis=2, concat_axis=0, t...  18.8 us
    dot_general x1, matrix products, per_device(): jnp.dot(lax.all_gather(value_vectors, ('role', 'seq'), axis=0, tiled=True...  7.84 us
    psum x1, blocking collectives, per_device(): sumsq = lax.psum(jnp.sum(resid * resid, axis=1), ('role', 'seq'))  5.66 us
    all_gather x1, blocking collectives, per_device(): lax.all_gather(value_vectors, ('role', 'seq'), axis=0, tiled=True)  5.41 us
  transfers between devices with their start and end apart: 7, of which 6 were waited for; matrix products, arithmetic and copies ran while one was open for 8% of the time, Pallas kernels for 0%

commit v1 on v0

--- a/solution.py
+++ b/solution.py
@@ -98,7 +98,7 @@
     )
     gate_term = jnp.dot(normed, gate_weight, preferred_element_type=jnp.float32)
     up_term = jnp.dot(normed, up_weight, preferred_element_type=jnp.float32)
-    gate, up = lax.psum((gate_term, up_term), ("role", "seq"))
+    gate, up = lax.psum(lax.psum((gate_term, up_term), "seq"), "role")
     hidden = (jax.nn.silu(gate) * up).astype(jnp.bfloat16)
     rows_here = resid.shape[0] // lax.axis_size("ctx")
     ffn_rows = lax.psum_scatter(

time: 228 us -> 241 us (1.057)
  waiting for transfers between devices: 125 us -> 138 us
    psum x1 -> x2, waiting for transfers between devices: 32.9 us -> 45.8 us  [per_device(): gate, up = lax.psum(lax.psum((gate_term, up_term), 'seq'), 'role')]
    unnamed x5 -> x6, waiting for transfers between devices: 34 us -> 34 us
  transfers between devices with their start and end apart: 7 -> 8, of which waited for: 6 -> 7; matrix products, arithmetic and copies ran while one was open for 8% -> 7% of each run, Pallas kernels for 0% -> 0%
where the time goes in v1:
time: 241 us; the launch traced here: 240 us
  waiting for transfers between devices  138 us (57%)
  blocking collectives  31 us (13%)
  matrix products  30.2 us (13%)
  between operations  14 us (6%)
  starting transfers between devices  10.7 us (4%)
  other arithmetic  9.47 us (4%)
  local copies, waits for them, and re-layouts  6.56 us (3%)
    psum x2, waiting for transfers between devices, per_device(): gate, up = lax.psum(lax.psum((gate_term, up_term), 'seq'), 'role')  45.8 us
    unnamed x6, waiting for transfers between devices  34 us
    psum x1, waiting for transfers between devices, per_device(): attn_out = lax.psum(per_head_terms, 'ctx')  33.5 us
    all_gather x1, blocking collectives, per_device(): all_heads = lax.all_gather(queries, 'ctx', axis=1, tiled=True)  19.9 us
    all_to_all x1, waiting for transfers between devices, per_device(): lax.all_to_all(partial_value[None], 'ctx', split_axis=2, concat_axis=0, t...  18.8 us
    dot_general x1, matrix products, per_device(): jnp.dot(lax.all_gather(value_vectors, ('role', 'seq'), axis=0, tiled=True...  7.84 us
    psum x1, blocking collectives, per_device(): sumsq = lax.psum(jnp.sum(resid * resid, axis=1), ('role', 'seq'))  5.66 us
    all_gather x1, blocking collectives, per_device(): lax.all_gather(value_vectors, ('role', 'seq'), axis=0, tiled=True)  5.41 us
  transfers between devices with their start and end apart: 8, of which 7 were waited for; matrix products, arithmetic and copies ran while one was open for 7% of the time, Pallas kernels for 0%

profile of v1, /device:TPU:0, one launch (start us, length us, event | category | flops | bytes accessed | tf_op | source)
XLA Modules:
  0.0 240.1 jit_solution(9200819351560369629)
XLA Ops:
  6.5 0.7 all-gather.3.cloned.1.call-update
  7.3 1.3 fusion.19
  8.6 1.3 fusion.12
  9.9 19.9 %all_gather.9 = bf16[4,128,576]{2,1,0:T(8,128)(2,1)S(1)} all-gather(bf16[4,32,576]{2,1,0:T(8,128)(2,1)} %param.11), channel_id=1, replica_groups=mesh['groups'=2,'ctx'=4,'role'=2,'seq'=2] {'ctx'}, dimensions={1}, use_global_device_ids=true | all-gather | bytes 737280 | tf_op jit(solution)/shard_map/all_gather | solution.py:38
  29.8 0.8 fusion.20
  30.7 1.8 convolution_multiply_fusion
  32.6 0.9 select_reduce_fusion.1
  33.5 0.9 convert_reduce_fusion.1
  35.1 0.8 reduce.1
  35.9 0.7 reshape.68
  36.6 3.8 %all-to-all-start.2 = ((f32[4,1,128]{2,1,0:T(1,128)}), f32[4,1,128]{2,1,0:T(1,128)S(1)}, u32[]{:S(2)}, u32[]{:S(2)}) async-start(f32[4,1,128]{2,1,0:T(1,128)} %reshape.68), calls=%async_computation.2 | async-start | bytes 4096 | tf_op jit(solution)/shard_map/all_to_all | solution.py:77
  41.7 0.8 reduce.3
  42.5 0.7 reshape.66
  44.0 1.9 all-to-all-done.2
  45.9 3.2 %all-to-all-start = ((f32[4,1,128]{2,1,0:T(1,128)}), f32[4,1,128]{2,1,0:T(1,128)S(1)}, u32[]{:S(2)}, u32[]{:S(2)}) async-start(f32[4,1,128]{2,1,0:T(1,128)} %reshape.66), calls=%async_computation | async-start | bytes 4096 | tf_op jit(solution)/shard_map/all_to_all | solution.py:76
  49.1 1.4 maximum_bitcast_fusion
  50.6 4.1 %all-to-all-done = f32[4,1,128]{2,1,0:T(1,128)S(1)} async-done(((f32[4,1,128]{2,1,0:T(1,128)}), f32[4,1,128]{2,1,0:T(1,128)S(1)}, u32[]{:S(2)}, u32[]{:S(2)}) %all-to-all-start) | async-done | bytes 2080 | tf_op jit(solution)/shard_map/all_to_all | solution.py:76
  54.7 3.5 %all-to-all-start.1 = ((f32[1,4,128,512]{3,1,0,2:T(4,128)}), f32[1,4,128,512]{3,1,0,2:T(4,128)S(1)}, u32[]{:S(2)}, u32[]{:S(2)}) async-start(f32[1,4,128,512]{3,1,0,2:T(4,128)} %maximum_bitcast_fusion), calls=%async_computation.1 | async-start | bytes 2097152 | tf_op jit(solution)/shard_map/all_to_all | solution.py:78
  60.1 18.8 %all-to-all-done.1 = f32[1,4,128,512]{3,1,0,2:T(4,128)S(1)} async-done(((f32[1,4,128,512]{3,1,0,2:T(4,128)}), f32[1,4,128,512]{3,1,0,2:T(4,128)S(1)}, u32[]{:S(2)}, u32[]{:S(2)}) %all-to-all-start.1) | async-done | bytes 1048608 | tf_op jit(solution)/shard_map/all_to_all | solution.py:78
  79.4 2.8 %fusion = bf16[1,4,4096]{2,1,0:T(4,128)(2,1)S(1)} fusion(bf16[32,512,128]{2,1,0:T(8,128)(2,1)} %all-gather.3.cloned.1.call-done, bf16[4,32,512]{2,1,0:T(8,128)(2,1)S(1)} %divide_convert_fusion), kind=kOutput, calls=%fused_computation.5 | convolution fusion | flops 16793600 | bytes 4358144 | tf_op jit(solution)/shard_map/nut,utc->nuc/dot_general | solution.py:81
  82.2 5.4 %all-gather = bf16[4,4,4096]{2,1,0:T(4,128)(2,1)S(1)} all-gather(bf16[1,4,4096]{2,1,0:T(4,128)(2,1)S(1)} %fusion), channel_id=1, replica_groups=mesh['groups'=2,'ctx'=4,'role'=2,'seq'=2] {'role','seq'}, dimensions={0}, use_global_device_ids=true | all-gather | bytes 163840 | tf_op jit(solution)/shard_map/all_gather | solution.py:89
  87.7 7.8 %fusion.21 = f32[16,1792]{1,0:T(8,128)} fusion(bf16[16,4096]{1,0:T(8,128)(2,1)S(1)} %reshape.63, bf16[4096,1792]{1,0:T(8,128)(2,1)} %param.16), kind=kOutput, calls=%fused_computation.50 | convolution fusion | flops 234881024 | bytes 14925824 | tf_op jit(solution)/shard_map/dot_general | solution.py:88
  95.6 33.5 %all-reduce.8.cloned.1.call-done = f32[16,1792]{1,0:T(8,128)} async-done(((f32[16,1792]{1,0:T(8,128)}), f32[16,1792]{1,0:T(8,128)}) %all-reduce.8.cloned.1.call-update) | async-done | bytes 114704 | tf_op jit(solution)/shard_map/psum | solution.py:93
  129.1 1.0 multiply_reduce_fusion
  130.1 5.7 %psum.43 = f32[16]{0:T(128)S(1)} all-reduce(f32[16]{0:T(128)S(1)} %get-tuple-element.11), channel_id=1, replica_groups=mesh['groups'=2,'ctx'=4,'role'=2,'seq'=2] {'role','seq'}, use_global_device_ids=true, to_apply=%region_9.10 | all-reduce | flops 16 | bytes 128 | tf_op jit(solution)/shard_map/psum | solution.py:95
  135.8 5.2 %fusion.16 = f32[16,2304]{1,0:T(8,128)} fusion(bf16[1792,2304]{1,0:T(8,128)(2,1)} %param.19, f32[16,1792]{1,0:T(8,128)S(1)} %get-tuple-element.12, f32[1792]{0:T(1024)S(1)} %copy-done.1, f32[16]{0:T(128)S(1)} %add_rsqrt_fusion), kind=kOutput, calls=%fused_computation.46 | convolution fusion | flops 132206592 | bytes 8526912 | tf_op jit(solution)/shard_map/dot_general | solution.py:99
  141.1 5.3 %fusion.15 = f32[16,2304]{1,0:T(8,128)} fusion(bf16[1792,2304]{1,0:T(8,128)(2,1)} %param.20, f32[16,1792]{1,0:T(8,128)S(1)} %get-tuple-element.12, f32[1792]{0:T(1024)S(1)} %copy-done.1, f32[16]{0:T(128)S(1)} %add_rsqrt_fusion), kind=kOutput, calls=%fused_computation.45 | convolution fusion | flops 132206592 | bytes 8526912 | tf_op jit(solution)/shard_map/dot_general | solution.py:100
  146.4 18.7 %all-reduce.12.cloned.1.call-done = (f32[16,2304]{1,0:T(8,128)}, f32[16,2304]{1,0:T(8,128)}) async-done(((f32[16,2304]{1,0:T(8,128)}, f32[16,2304]{1,0:T(8,128)}), (f32[16,2304]{1,0:T(8,128)}, f32[16,2304]{1,0:T(8,128)})) %all-reduce.12.cloned.1.call-update) | async-done | bytes 294928 | tf_op jit(solution)/shard_map/psum | solution.py:101
  165.2 27.1 %all-reduce.14.cloned.1.call-done = (f32[16,2304]{1,0:T(8,128)}, f32[16,2304]{1,0:T(8,128)}) async-done(((f32[16,2304]{1,0:T(8,128)}, f32[16,2304]{1,0:T(8,128)}), (f32[16,2304]{1,0:T(8,128)}, f32[16,2304]{1,0:T(8,128)})) %all-reduce.14.cloned.1.call-update) | async-done | bytes 294928 | tf_op jit(solution)/shard_map/psum | solution.py:101
  192.3 5.4 %fusion.7 = f32[16,1792]{1,0:T(8,128)} fusion(bf16[2304,1792]{1,0:T(8,128)(2,1)} %param.21, f32[16,2304]{1,0:T(8,128)} %get-tuple-element.9, f32[16,2304]{1,0:T(8,128)} %get-tuple-element.10), kind=kOutput, calls=%fused_computation.27 | convolution fusion | flops 132341760 | bytes 8667136 | tf_op jit(solution)/shard_map/dot_general | solution.py:105
  198.9 33.2 %all-reduce.10.cloned.1.call-done = f32[16,1792]{1,0:T(8,128)} async-done(((f32[16,1792]{1,0:T(8,128)}), f32[16,1792]{1,0:T(8,128)}) %all-reduce.10.cloned.1.call-update) | async-done | bytes 114704
  232.2 1.4 fusion.9
  (44 shorter events, 6.1 us)
Async XLA Ops:
  6.5 26.1 %copy-start = (bf16[2,1024,576]{1,2,0:T(8,128)(2,1)S(1)}, bf16[2,1024,576]{1,2,0:T(8,128)(2,1)}, u32[]{:S(2)}) copy-start(bf16[2,1024,576]{1,2,0:T(8,128)(2,1)} %param.12) | copy-start | bytes 7077892
  6.5 72.8 %all-gather.3.cloned.1.call-start = ((), (), s32[]{:S(2)}) async-start(), calls=%async_computation.3 | async-start | bytes 5242880 | tf_op jit(solution)/shard_map/all_gather | solution.py:84
  36.6 9.3 %all-to-all-start.2 = ((f32[4,1,128]{2,1,0:T(1,128)}), f32[4,1,128]{2,1,0:T(1,128)S(1)}, u32[]{:S(2)}, u32[]{:S(2)}) async-start(f32[4,1,128]{2,1,0:T(1,128)} %reshape.68), calls=%async_computation.2 | async-start | bytes 4096 | tf_op jit(solution)/shard_map/all_to_all | solution.py:77
  45.9 8.8 %all-to-all-start = ((f32[4,1,128]{2,1,0:T(1,128)}), f32[4,1,128]{2,1,0:T(1,128)S(1)}, u32[]{:S(2)}, u32[]{:S(2)}) async-start(f32[4,1,128]{2,1,0:T(1,128)} %reshape.66), calls=%async_computation | async-start | bytes 4096 | tf_op jit(solution)/shard_map/all_to_all | solution.py:76
  54.7 24.2 %all-to-all-start.1 = ((f32[1,4,128,512]{3,1,0,2:T(4,128)}), f32[1,4,128,512]{3,1,0,2:T(4,128)S(1)}, u32[]{:S(2)}, u32[]{:S(2)}) async-start(f32[1,4,128,512]{3,1,0,2:T(4,128)} %maximum_bitcast_fusion), calls=%async_computation.1 | async-start | bytes 2097152 | tf_op jit(solution)/shard_map/all_to_all | solution.py:78
  58.2 70.9 %all-reduce.8.cloned.1.call-start = ((), (), s32[]{:S(2)}) async-start(), calls=%async_computation.4 | async-start | bytes 229376 | tf_op jit(solution)/shard_map/psum | solution.py:93
  87.7 41.4 %copy-start.2 = (bf16[16,1792]{1,0:T(8,128)(2,1)S(1)}, bf16[16,1792]{1,0:T(8,128)(2,1)}, u32[]{:S(2)}) copy-start(bf16[16,1792]{1,0:T(8,128)(2,1)} %param.17) | copy-start | bytes 172036
  87.7 48.1 %copy-start.1 = (f32[1792]{0:T(1024)S(1)}, f32[1792]{0:T(1024)}, u32[]{:S(2)}) copy-start(f32[1792]{0:T(1024)} %param.18) | copy-start | bytes 21508
  95.6 69.5 %all-reduce.12.cloned.1.call-start = ((), (), s32[]{:S(2)}) async-start(), calls=%async_computation.6 | async-start | bytes 589824 | tf_op jit(solution)/shard_map/psum | solution.py:101
  146.3 46.0 %all-reduce.14.cloned.1.call-start = ((), (), s32[]{:S(2)}) async-start(), calls=%async_computation.7 | async-start | bytes 589824 | tf_op jit(solution)/shard_map/psum | solution.py:101
  165.1 67.1 %all-reduce.10.cloned.1.call-start = ((), (), s32[]{:S(2)}) async-start(), calls=%async_computation.5 | async-start | bytes 229376
  192.3 5.4 %copy-start.3 = (u32[32]{0:T(128)S(1)}, u32[32]{0:T(128)}, u32[]{:S(2)}) copy-start(u32[32]{0:T(128)} %constant.35) | copy-start | bytes 388
Sparse Core Ops, SparseCore 0:
  8.9 37.1 all-gather.2
  95.7 33.3 all-reduce.7
  146.4 18.5 all-reduce.11
  167.3 24.9 all-reduce.13
  197.8 34.3 all-reduce.9
